TPU v7x, 32 devices: a whole 2x2x4 slice. The times are simulated.
32 devices in a mesh: row: 8 (over z, y), basis: 4 (over x, core).
Axes of the slice: x: 2, y: 2, z: 4, core: 2. Of those that a mesh axis runs over, the one named last changes fastest.
Arguments:
- design: float32 [7680, 40960], P('row', 'basis'), may hold values from -0.029646354 to 0.029646354
- targets: float32 [7680], P('row'), may hold values from -6 to 6
- counts: int32 [7680, 128], P('row'), may hold values from 0 to 3
- coefficients: float32 [40960, 128], P('basis'), may hold values from -6 to 6
- step_size: float32 [128], replicated, may hold values from 0.03 to 0.15
Outputs:
- fitted: float32 [40960, 128], P('basis')
- influence: float32 [7680, 128], P('row')
All inputs are finite; a program needn't handle non-finite values.
Results may differ from a plain program's by a relative error of at most 0.00017.
Values sent between devices are 32-bit elements; how exact they have to be, the bound alone decides.
No kernel may reach another device: no remote copies, remote signals or barrier semaphores. Data moves between devices by JAX's collectives and lax.ppermute only.
A program may use at most 128 MiB of HBM per device.

v0:
```python
import jax
import jax.numpy as jnp
from jax import lax
from jax.sharding import PartitionSpec as P

STEPS = 3


HIGH = lax.Precision.HIGHEST


def transposed(left, right):
    return lax.dot_general(
        left, right, (((0,), (0,)), ((), ())), precision=HIGH, preferred_element_type=jnp.float32
    )


def predictions(partial_value):
    return lax.psum(partial_value, "basis")


def weighted(predicted, targets, weights):
    residual = predicted - targets[:, None]
    return weights * residual / jnp.sqrt(1.0 + residual * residual)


def shards(design, targets, counts, coefficients, step_size):
    weights = counts.astype(jnp.float32)
    curve_term = transposed(design * design, weights)
    influence = jnp.zeros((design.shape[0], coefficients.shape[1]), jnp.float32)
    share_rows = coefficients.shape[0] // lax.axis_size("row")
    offset = lax.axis_index("row") * share_rows
    curvature = lax.psum_scatter(curve_term, "row", scatter_dimension=0, tiled=True) + 0.01
    share = lax.dynamic_slice_in_dim(coefficients, offset, share_rows, 0)
    for step in range(STEPS):
        if step == 0:
            partial_value = jnp.dot(
                design, coefficients, precision=HIGH, preferred_element_type=jnp.float32
            )
        else:
            partial_value = jnp.dot(
                design,
                lax.all_gather(share, "row", axis=0, tiled=True),
                precision=HIGH,
                preferred_element_type=jnp.float32,
            )
        influence = weighted(predictions(partial_value), targets, weights)
        gradient = lax.psum_scatter(
            transposed(design, influence), "row", scatter_dimension=0, tiled=True
        )
        share = share - step_size[None, :] * gradient / curvature
    fitted = lax.all_gather(share, "row", axis=0, tiled=True)
    return (fitted, influence)


def solution(mesh):
    return jax.shard_map(
        shards,
        mesh=mesh,
        in_specs=(P("row", "basis"), P("row"), P("row", None), P("basis", None), P()),
        out_specs=(P("basis", None), P("row", None)),
        check_vma=False,
    )
```

profile of v0, /device:TPU:0, one launch (start us, length us, event | category | flops | bytes accessed | tf_op | source)
XLA Modules:
  0.0 961.2 jit_solution(473307508805316564)
XLA Ops:
  8.0 0.0 copy-start
  8.0 0.0 all-reduce.4.cloned.1.call-start
  8.1 35.6 %fusion.23 = f32[960,128]{1,0:T(8,128)} fusion(f32[960,10240]{1,0:T(8,128)} %param.5, f32[10240,128]{1,0:T(8,128)} %param.8), kind=kOutput, calls=%fused_computation.33 | convolution fusion | flops 15099494400 | bytes 45056000 | tf_op jit(solution)/shard_map/dot_general | solution.py:37
  43.6 0.0 copy-start.5
  43.6 0.0 all-reduce.4.cloned.1.call-update
  43.6 0.0 reduce-scatter.7.cloned.1.call-start
  43.7 0.0 copy-done
  43.7 29.3 %fusion = f32[10240,128]{0,1:T(8,128)} fusion(f32[960,10240]{1,0:T(8,128)} %param.5, s32[960,128]{1,0:T(8,128)S(1)} %copy-done), kind=kOutput, calls=%fused_computation | convolution fusion | flops 15109447680 | bytes 45056000 | tf_op jit(solution)/shard_map/dot_general | solution.py:13
  73.0 0.0 reduce-scatter.7.cloned.1.call-update
  73.1 0.0 copy-start.6
  73.1 0.6 reduce-scatter.5.cloned.1.call-start
  73.6 6.2 all-reduce.4.cloned.1.call-done
  79.8 0.0 copy-done.5
  79.8 29.3 %convolution_bitcast_fusion.2 = f32[10240,128]{0,1:T(8,128)} fusion(f32[960,10240]{1,0:T(8,128)} %param.5, f32[960,128]{1,0:T(8,128)} %all-reduce.4.cloned.1.call-done, s32[960,128]{1,0:T(8,128)S(1)} %copy-done, f32[960]{0:T(1024)S(1)} %copy-done.5), kind=kOutput, calls=%fused_computation.4 | convolution fusion | flops 15100231680 | bytes 45551360 | tf_op jit(solution)/shard_map/dot_general | solution.py:13
  109.1 0.0 reduce-scatter.5.cloned.1.call-update
  109.1 0.0 all-gather.4.cloned.1.call-start
  109.2 1.1 constant_dynamic-slice_fusion
  110.3 0.2 copy.11
  110.6 68.3 %reduce-scatter.7.cloned.1.call-done = f32[1280,128]{0,1:T(8,128)} async-done(((f32[10240,128]{0,1:T(8,128)}), f32[1280,128]{0,1:T(8,128)}) %reduce-scatter.7.cloned.1.call-update) | async-done | bytes 655376 | tf_op jit(solution)/shard_map/reduce_scatter | solution.py:33
  178.9 106.6 %reduce-scatter.5.cloned.1.call-done = f32[1280,128]{0,1:T(8,128)} async-done(((f32[10240,128]{0,1:T(8,128)}), f32[1280,128]{0,1:T(8,128)}) %reduce-scatter.5.cloned.1.call-update) | async-done | bytes 655376 | tf_op jit(solution)/shard_map/reduce_scatter | solution.py:48
  285.5 0.0 copy-done.6
  285.5 2.3 divide_subtract_fusion.2
  287.8 0.0 all-gather.4.cloned.1.call-update
  287.8 0.2 all-reduce.6.cloned.1.call-start
  288.0 85.1 %all-gather.4.cloned.1.call-done = f32[10240,128]{0,1:T(8,128)} async-done(((f32[1280,128]{0,1:T(8,128)}), f32[10240,128]{0,1:T(8,128)}) %all-gather.4.cloned.1.call-update) | async-done | bytes 5242896 | tf_op jit(solution)/shard_map/all_gather | solution.py:43
  373.2 35.7 %convolution_bitcast_fusion.4 = f32[960,128]{1,0:T(8,128)} fusion(f32[10240,128]{0,1:T(8,128)} %all-gather.4.cloned.1.call-done, f32[960,10240]{1,0:T(8,128)} %param.5), kind=kOutput, calls=%fused_computation.6 | convolution fusion | flops 15099494400 | bytes 45056000 | tf_op jit(solution)/shard_map/dot_general | solution.py:41
  408.8 0.0 copy-start.2
  408.8 0.0 copy-start.3
  408.8 0.0 all-reduce.6.cloned.1.call-update
  408.8 0.3 reduce-scatter.9.cloned.1.call-start
  409.1 31.5 %all-reduce.6.cloned.1.call-done = f32[960,128]{1,0:T(8,128)} async-done(((f32[960,128]{1,0:T(8,128)}), f32[960,128]{1,0:T(8,128)}) %all-reduce.6.cloned.1.call-update) | async-done | bytes 491536 | tf_op jit(solution)/shard_map/psum | solution.py:19
  440.6 29.0 %convolution_bitcast_fusion.1 = f32[10240,128]{0,1:T(8,128)} fusion(f32[960,10240]{1,0:T(8,128)} %param.5, f32[960,128]{1,0:T(8,128)} %all-reduce.6.cloned.1.call-done, s32[960,128]{1,0:T(8,128)S(1)} %copy-done, f32[960]{0:T(1024)S(1)} %copy-done.5), kind=kOutput, calls=%fused_computation.3 | convolution fusion | flops 15100231680 | bytes 45551360 | tf_op jit(solution)/shard_map/dot_general | solution.py:13
  469.6 0.0 reduce-scatter.9.cloned.1.call-update
  469.6 0.0 all-gather.6.cloned.1.call-start
  469.6 103.1 %reduce-scatter.9.cloned.1.call-done = f32[1280,128]{0,1:T(8,128)} async-done(((f32[10240,128]{0,1:T(8,128)}), f32[1280,128]{0,1:T(8,128)}) %reduce-scatter.9.cloned.1.call-update) | async-done | bytes 655376 | tf_op jit(solution)/shard_map/reduce_scatter | solution.py:48
  572.7 0.0 copy-done.2
  572.7 0.0 copy-done.3
  572.7 2.1 divide_subtract_fusion.1
  574.8 0.0 all-gather.6.cloned.1.call-update
  574.9 0.3 all-reduce.8.cloned.1.call-start
  575.2 85.0 %all-gather.6.cloned.1.call-done = f32[10240,128]{0,1:T(8,128)} async-done(((f32[1280,128]{0,1:T(8,128)}), f32[10240,128]{0,1:T(8,128)}) %all-gather.6.cloned.1.call-update) | async-done | bytes 5242896 | tf_op jit(solution)/shard_map/all_gather | solution.py:43
  660.2 35.7 %convolution_bitcast_fusion.3 = f32[960,128]{1,0:T(8,128)} fusion(f32[10240,128]{0,1:T(8,128)} %all-gather.6.cloned.1.call-done, f32[960,10240]{1,0:T(8,128)} %param.5), kind=kOutput, calls=%fused_computation.5 | convolution fusion | flops 15099494400 | bytes 45056000 | tf_op jit(solution)/shard_map/dot_general | solution.py:41
  695.8 0.0 copy-start.1
  695.8 0.0 all-reduce.8.cloned.1.call-update
  695.9 0.3 reduce-scatter.11.cloned.1.call-start
  696.2 31.4 %all-reduce.8.cloned.1.call-done = f32[960,128]{1,0:T(8,128)} async-done(((f32[960,128]{1,0:T(8,128)}), f32[960,128]{1,0:T(8,128)}) %all-reduce.8.cloned.1.call-update) | async-done | bytes 491536 | tf_op jit(solution)/shard_map/psum | solution.py:19
  727.6 1.2 rsqrt_multiply_fusion
  728.8 0.0 copy-start.4
  728.9 27.8 %convolution_bitcast_fusion = f32[10240,128]{0,1:T(8,128)} fusion(f32[960,128]{1,0:T(8,128)S(1)} %rsqrt_multiply_fusion, f32[960,10240]{1,0:T(8,128)} %param.5), kind=kOutput, calls=%fused_computation.2 | convolution fusion | flops 15099494400 | bytes 45056000 | tf_op jit(solution)/shard_map/dot_general | solution.py:13
  756.7 0.0 reduce-scatter.11.cloned.1.call-update
  756.7 0.0 all-gather.8.cloned.1.call-start
  756.8 103.1 %reduce-scatter.11.cloned.1.call-done = f32[1280,128]{0,1:T(8,128)} async-done(((f32[10240,128]{0,1:T(8,128)}), f32[1280,128]{0,1:T(8,128)}) %reduce-scatter.11.cloned.1.call-update) | async-done | bytes 655376 | tf_op jit(solution)/shard_map/reduce_scatter | solution.py:48
  859.8 0.0 copy-done.1
  859.8 2.1 divide_subtract_fusion
  861.9 0.0 all-gather.8.cloned.1.call-update
  861.9 85.8 %all-gather.8.cloned.1.call-done = f32[10240,128]{0,1:T(8,128)} async-done(((f32[1280,128]{0,1:T(8,128)}), f32[10240,128]{0,1:T(8,128)}) %all-gather.8.cloned.1.call-update) | async-done | bytes 5242896 | tf_op jit(solution)/shard_map/all_gather | solution.py:52
  947.7 5.9 copy.9
  953.6 0.0 copy-done.4
Async XLA Ops:
  8.0 35.7 %copy-start = (s32[960,128]{1,0:T(8,128)S(1)}, s32[960,128]{1,0:T(8,128)}, u32[]{:S(2)}) copy-start(s32[960,128]{1,0:T(8,128)} %param.7) | copy-start | bytes 1474564
  8.0 71.8 %all-reduce.4.cloned.1.call-start = ((), (), s32[]{:S(2)}) async-start(), calls=%async_computation.4 | async-start | bytes 983040 | tf_op jit(solution)/shard_map/psum | solution.py:19
  43.6 36.2 %copy-start.5 = (f32[960]{0:T(1024)S(1)}, f32[960]{0:T(1024)}, u32[]{:S(2)}) copy-start(f32[960]{0:T(1024)} %param.6) | copy-start | bytes 11524
  43.6 135.2 %reduce-scatter.7.cloned.1.call-start = ((), (), s32[]{:S(2)}) async-start(), calls=%async_computation.6 | async-start | bytes 5898240 | tf_op jit(solution)/shard_map/reduce_scatter | solution.py:33
  73.1 212.4 %copy-start.6 = (f32[128]{0:T(128)S(1)}, f32[128]{0:T(128)}, u32[]{:S(2)}) copy-start(f32[128]{0:T(128)} %param.9) | copy-start | bytes 1540
  73.1 212.4 %reduce-scatter.5.cloned.1.call-start = ((), (), s32[]{:S(2)}) async-start(), calls=%async_computation.5 | async-start | bytes 5898240 | tf_op jit(solution)/shard_map/reduce_scatter | solution.py:48
  109.1 264.0 %all-gather.4.cloned.1.call-start = ((), (), s32[]{:S(2)}) async-start(), calls=%async_computation.7 | async-start | bytes 5898240 | tf_op jit(solution)/shard_map/all_gather | solution.py:43
  287.8 152.8 %all-reduce.6.cloned.1.call-start = ((), (), s32[]{:S(2)}) async-start(), calls=%async_computation.8 | async-start | bytes 983040 | tf_op jit(solution)/shard_map/psum | solution.py:19
  408.8 163.9 %copy-start.2 = (f32[1280,128]{0,1:T(8,128)S(1)}, f32[1280,128]{0,1:T(8,128)}, u32[]{:S(2)}) copy-start(f32[1280,128]{0,1:T(8,128)} %divide_subtract_fusion.2) | copy-start | bytes 1966084
  408.8 163.9 %copy-start.3 = (f32[1280,128]{0,1:T(8,128)S(1)}, f32[1280,128]{0,1:T(8,128)}, u32[]{:S(2)}) copy-start(f32[1280,128]{0,1:T(8,128)} %reduce-scatter.7.cloned.1.call-done) | copy-start | bytes 1966084
  408.8 163.9 %reduce-scatter.9.cloned.1.call-start = ((), (), s32[]{:S(2)}) async-start(), calls=%async_computation.9 | async-start | bytes 5898240 | tf_op jit(solution)/shard_map/reduce_scatter | solution.py:48
  469.6 190.6 %all-gather.6.cloned.1.call-start = ((), (), s32[]{:S(2)}) async-start(), calls=%async_computation.10 | async-start | bytes 5898240 | tf_op jit(solution)/shard_map/all_gather | solution.py:43
  574.9 152.8 %all-reduce.8.cloned.1.call-start = ((), (), s32[]{:S(2)}) async-start(), calls=%async_computation.11 | async-start | bytes 983040 | tf_op jit(solution)/shard_map/psum | solution.py:19
  695.8 164.0 %copy-start.1 = (f32[1280,128]{0,1:T(8,128)S(1)}, f32[1280,128]{0,1:T(8,128)}, u32[]{:S(2)}) copy-start(f32[1280,128]{0,1:T(8,128)} %divide_subtract_fusion.1) | copy-start | bytes 1966084
  695.9 163.9 %reduce-scatter.11.cloned.1.call-start = ((), (), s32[]{:S(2)}) async-start(), calls=%async_computation.12 | async-start | bytes 5898240 | tf_op jit(solution)/shard_map/reduce_scatter | solution.py:48
  728.8 224.7 %copy-start.4 = (f32[960,128]{1,0:T(8,128)}, f32[960,128]{1,0:T(8,128)S(1)}, u32[]{:S(2)}) copy-start(f32[960,128]{1,0:T(8,128)S(1)} %rsqrt_multiply_fusion) | copy-start | bytes 1474564
  756.7 191.0 %all-gather.8.cloned.1.call-start = ((), (), s32[]{:S(2)}) async-start(), calls=%async_computation.13 | async-start | bytes 5898240 | tf_op jit(solution)/shard_map/all_gather | solution.py:52
Sparse Core Ops, SparseCore 0:
  43.8 36.0 all-reduce.3
  409.0 31.5 all-reduce.5
  696.0 31.5 all-reduce.7
Sparse Core Ops, SparseCore 1:
  73.1 105.7 reduce-scatter.6
  182.9 102.5 reduce-scatter.4
  287.9 85.2 all-gather.3
  469.7 103.0 reduce-scatter.8
  574.9 85.2 all-gather.5
  756.8 103.0 reduce-scatter.10
  862.5 85.2 all-gather.7
where the time goes:
time: 969 us; the launch traced here: 961 us
  waiting for transfers between devices  706 us (73%)
  matrix products  222 us (23%)
  between operations  15.9 us (2%)
    reduce_scatter x3, waiting for transfers between devices, shards(): lax.psum_scatter(transposed(design, influence), 'row', scatter_dimension=...  313 us
    all_gather x2, waiting for transfers between devices, shards(): lax.all_gather(share, 'row', axis=0, tiled=True)  170 us
    dot_general x4, matrix products, transposed(): lax.dot_general(left, right, (((0,), (0,)), ((), ())), precision=HIGH, pr...  115 us
    all_gather x1, waiting for transfers between devices, shards(): fitted = lax.all_gather(share, 'row', axis=0, tiled=True)  85.8 us
    dot_general x2, matrix products, shards(): jnp.dot(design, lax.all_gather(share, 'row', axis=0, tiled=True), precisi...  71.3 us
    psum x3, waiting for transfers between devices, predictions(): return lax.psum(partial_value, 'basis')  69 us
    reduce_scatter x1, waiting for transfers between devices, shards(): lax.psum_scatter(curve_term, 'row', scatter_dimension=0, tiled=True) + 0.01  68.3 us
    dot_general x1, matrix products, shards(): jnp.dot(design, coefficients, precision=HIGH, preferred_element_type=jnp....  35.6 us
  transfers between devices with their start and end apart: 10, of which 10 were waited for; matrix products, arithmetic and copies ran while one was open for 6% of the time, Pallas kernels for 0%

commit v1 on v0

v1 whole, which is shorter than its diff:
```python
import functools

import jax
import jax.numpy as jnp
from jax import lax
from jax.experimental import pallas as pl
from jax.experimental.pallas import tpu as pltpu
from jax.sharding import PartitionSpec as P


STEPS = 3
OFFLOADED = 0.55
TILE = 512
DEPTH = 4


LIMIT = 40 * 1024 * 1024


def halves(value):
    high = value.astype(jnp.bfloat16)
    low = (value - high.astype(jnp.float32)).astype(jnp.bfloat16)
    return high, low


def dot(left, right):
    return jnp.dot(left, right, preferred_element_type=jnp.float32)


def cost_of(rows, columns, members):
    return pl.CostEstimate(
        flops=8 * rows * columns * members,
        bytes_accessed=4 * (rows * columns + columns * members + rows * members),
        transcendentals=0,
    )


def stream_scratch(rows, tile):
    return [pltpu.VMEM((DEPTH, rows, tile), jnp.float32), pltpu.SemaphoreType.DMA((DEPTH,))]


def stream(design, buffer, arrived, first, steps):
    tile = buffer.shape[2]
    step = pl.program_id(0)

    def fetch(k):
        slot = lax.rem(k, DEPTH)
        return pltpu.make_async_copy(
            design.at[:, pl.ds(pl.multiple_of(first + k * tile, 128), tile)],
            buffer.at[slot],
            arrived.at[slot],
        )

    @pl.when(step == 0)
    def _():
        for k in range(min(DEPTH - 1, steps)):
            fetch(k).start()

    @pl.when(step + DEPTH - 1 < steps)
    def _():
        fetch(step + DEPTH - 1).start()

    fetch(step).wait()
    return buffer[lax.rem(step, DEPTH)]


ANYWHERE = pl.BlockSpec(memory_space=pl.ANY)


def whole_block(array):
    return pl.BlockSpec(array.shape, lambda t: (0,) * array.ndim)


def predict_kernel(first, steps, has_start, fitted, design, extra, out, total, buffer, arrived):
    members = fitted.shape[1]
    step = pl.program_id(0)
    block = stream(design, buffer, arrived, first, steps)
    right = jnp.concatenate(halves(fitted[...]), axis=1)
    term = dot(
        jnp.concatenate(halves(block), axis=1), jnp.concatenate([right, right], axis=0)
    )

    @pl.when(step == 0)
    def _():
        total[...] = term

    @pl.when(step > 0)
    def _():
        total[...] += term

    @pl.when(step == steps - 1)
    def _():
        value = total[:, :members] + total[:, members:]
        out[...] = value + extra[...] if has_start else value


def predict(design, fitted, first, tile, start=None, after=None):
    rows, (columns, members) = design.shape[0], fitted.shape
    steps = columns // tile
    extra = after if start is None else start
    return pl.pallas_call(
        functools.partial(predict_kernel, first, steps, start is not None),
        grid=(steps,),
        in_specs=[
            pl.BlockSpec((tile, members), lambda t: (t, 0)),
            ANYWHERE,
            ANYWHERE if start is None else whole_block(start),
        ],
        out_specs=pl.BlockSpec((rows, members), lambda t: (0, 0)),
        out_shape=jax.ShapeDtypeStruct((rows, members), jnp.float32),
        scratch_shapes=[pltpu.VMEM((rows, 2 * members), jnp.float32)]
        + stream_scratch(rows, tile),
        compiler_params=pltpu.CompilerParams(vmem_limit_bytes=LIMIT),
        cost_estimate=cost_of(rows, columns, members),
        name="predict",
    )(fitted, design, extra)


def stacked(value):
    return jnp.concatenate(halves(jnp.concatenate([value, value], axis=0).T), axis=0)


def gradient_tile(left, block, members):
    both = dot(left, jnp.concatenate(halves(block), axis=0))
    if both.shape[0] == 2 * members:
        both = both[:members] + both[members:]
    return both.T


def start_kernel(
    first, steps, predicted, targets, counts, design, out, influence, left, buffer, arrived
):
    members = counts.shape[1]
    block = stream(design, buffer, arrived, first, steps)

    @pl.when(pl.program_id(0) == 0)
    def _():
        residual = predicted[...] - targets[...]
        value = (
            counts[...].astype(jnp.float32) * residual / jnp.sqrt(1.0 + residual * residual)
        )
        influence[...] = value
        left[...] = stacked(value)

    out[...] = gradient_tile(left[...], block, members)


def gradient_start(predicted, targets, counts, design, first, columns, tile):
    rows, members = counts.shape
    small = (predicted, targets, counts)
    steps = columns // tile
    return pl.pallas_call(
        functools.partial(start_kernel, first, steps),
        grid=(steps,),
        in_specs=[whole_block(e) for e in small] + [ANYWHERE],
        out_specs=[
            pl.BlockSpec((tile, members), lambda t: (t, 0)),
            pl.BlockSpec((rows, members), lambda t: (0, 0)),
            pl.BlockSpec((2 * members, 2 * rows), lambda t: (0, 0)),
        ],
        out_shape=[
            jax.ShapeDtypeStruct((columns, members), jnp.float32),
            jax.ShapeDtypeStruct((rows, members), jnp.float32),
            jax.ShapeDtypeStruct((2 * members, 2 * rows), jnp.bfloat16),
        ],
        scratch_shapes=stream_scratch(rows, tile),
        compiler_params=pltpu.CompilerParams(vmem_limit_bytes=LIMIT),
        cost_estimate=cost_of(rows, columns, members),
        name="gradient_start",
    )(*small, design)


def more_kernel(first, steps, left, design, out, buffer, arrived):
    block = stream(design, buffer, arrived, first, steps)
    out[...] = gradient_tile(left[...], block, out.shape[1])


def gradient_more(left, design, first, columns, tile):
    rows, members = design.shape[0], left.shape[0] // 2
    steps = columns // tile
    return pl.pallas_call(
        functools.partial(more_kernel, first, steps),
        grid=(steps,),
        in_specs=[whole_block(left), ANYWHERE],
        out_specs=pl.BlockSpec((tile, members), lambda t: (t, 0)),
        out_shape=jax.ShapeDtypeStruct((columns, members), jnp.float32),
        scratch_shapes=stream_scratch(rows, tile),
        compiler_params=pltpu.CompilerParams(vmem_limit_bytes=LIMIT),
        cost_estimate=cost_of(rows, columns, members),
        name="gradient_more",
    )(left, design)


def squares_kernel(first, steps, counts, design, after, out, left, buffer, arrived):
    block = stream(design, buffer, arrived, first, steps)

    @pl.when(pl.program_id(0) == 0)
    def _():
        weights = counts[...].astype(jnp.float32)
        left[...] = jnp.concatenate([weights, weights], axis=0).T.astype(jnp.bfloat16)

    out[...] = gradient_tile(left[...], block * block, out.shape[1])


def squares(counts, design, first, columns, tile, after):
    rows, members = counts.shape
    steps = columns // tile
    return pl.pallas_call(
        functools.partial(squares_kernel, first, steps),
        grid=(steps,),
        in_specs=[whole_block(counts), ANYWHERE, ANYWHERE],
        out_specs=pl.BlockSpec((tile, members), lambda t: (t, 0)),
        out_shape=jax.ShapeDtypeStruct((columns, members), jnp.float32),
        scratch_shapes=[pltpu.VMEM((members, 2 * rows), jnp.bfloat16)]
        + stream_scratch(rows, tile),
        compiler_params=pltpu.CompilerParams(vmem_limit_bytes=LIMIT),
        cost_estimate=cost_of(rows, columns, members),
        name="squares",
    )(counts, design, after)


def grid_of(count):
    outer = next(k for k in range(1, count + 1) if count % k == 0 and k * k >= count)
    return outer, count // outer


def piece(array, index, rows):
    return lax.dynamic_slice_in_dim(array, index * rows, rows, 0)


def outer_perm(outer, inner, k):
    return [
        (o * inner + i, (o + k) % outer * inner + i) for o in range(outer) for i in range(inner)
    ]


def inner_perm(outer, inner, k):
    return [
        (o * inner + i, o * inner + (i + k) % inner) for o in range(outer) for i in range(inner)
    ]


def scatter_stage(array, size, place, perm_of):
    rows = array.shape[0] // size
    total = piece(array, place, rows)
    arrived = [
        lax.ppermute(piece(array, (place + k) % size, rows), "row", perm_of(k))
        for k in range(1, size)
    ]
    for term in arrived:
        total = total + term
    return total


def gather_stage(own, size, place, perm_of):
    rows = own.shape[0]
    arrived = [lax.ppermute(own, "row", perm_of(k)) for k in range(1, size)]
    line = arrived[::-1] + [own] + arrived[::-1]
    return lax.dynamic_slice_in_dim(
        jnp.concatenate(line, 0), (size - 1 - place) * rows, size * rows, 0
    )


class Permuted:
    def __init__(self, count):
        self.outer, self.inner = grid_of(count)
        index = lax.axis_index("row")
        self.o, self.i = index // self.inner, index % self.inner
        self.count = count

    def scatter(self, array):
        array = scatter_stage(
            array, self.inner, self.i, lambda k: inner_perm(self.outer, self.inner, k)
        )
        return scatter_stage(
            array, self.outer, self.o, lambda k: outer_perm(self.outer, self.inner, k)
        )

    def gather(self, own):
        own = gather_stage(own, self.outer, self.o, lambda k: outer_perm(self.outer, self.inner, k))
        return gather_stage(
            own, self.inner, self.i, lambda k: inner_perm(self.outer, self.inner, k)
        )

    def share(self, array):
        return piece(array, self.i * self.outer + self.o, array.shape[0] // self.count)


class Offloaded:
    def __init__(self, count):
        self.count = count

    def scatter(self, array):
        return lax.psum_scatter(array, "row", scatter_dimension=0, tiled=True)

    def gather(self, own):
        return lax.all_gather(own, "row", axis=0, tiled=True)

    def share(self, array):
        return piece(array, lax.axis_index("row"), array.shape[0] // self.count)


def basis_sum(value):
    count = lax.axis_size("basis")
    if count & (count - 1) or count < 2 or value.shape[0] % 16:
        return lax.psum(value, "basis")
    place = lax.axis_index("basis") % 2
    half = value.shape[0] // 2

    def across(array, bit):
        return lax.ppermute(array, "basis", [(b, b ^ bit) for b in range(count)])

    own = piece(value, place, half) + across(piece(value, 1 - place, half), 1)
    bit = 2
    while bit < count:
        own = own + across(own, bit)
        bit *= 2
    other = across(own, 1)
    return jnp.where(
        place == 0, jnp.concatenate([own, other], 0), jnp.concatenate([other, own], 0)
    )


def shards(design, targets, counts, coefficients, step_size):
    rows = lax.axis_size("row")
    basis = coefficients.shape[0]
    tile = next(t for t in (TILE, 256, 128) if basis % (2 * t) == 0)
    cut = int(basis * OFFLOADED) // tile * tile
    bounds = [0, cut, cut + (basis - cut) // (2 * tile) * tile, basis]
    ways = [Offloaded(rows), Permuted(rows), Permuted(rows)]
    parts = [part for part in zip(bounds, bounds[1:], ways) if part[0] < part[1]]
    column = targets[:, None]
    squared = []
    for a, b, _ in parts:
        squared.append(
            squares(counts, design, a, b - a, tile, squared[-1] if squared else counts)
        )
    shares = [way.share(coefficients[a:b]) for a, b, way in parts]
    rates = []
    for step in range(STEPS):
        if step == 0:
            for term, (_, _, way) in zip(squared, parts):
                rates.append(step_size[None, :] / (way.scatter(term) + 0.01))
            partial_value = predict(design, coefficients, 0, tile, after=squared[-1])
        else:
            partial_value = None
            for whole, (a, _, _) in reversed(list(zip(pieces, parts))):
                partial_value = predict(design, whole, a, tile, start=partial_value, after=whole)
        predicted = basis_sum(partial_value)
        first, influence, left = gradient_start(
            predicted, column, counts, design, 0, cut, tile
        )
        terms = [first]
        for a, b, _ in parts[1:]:
            terms.append(gradient_more(left, design, a, b - a, tile))
        moved = []
        for index, (_, _, way) in list(enumerate(parts))[1:]:
            total = way.scatter(terms[index])
            moved.append(shares[index] - rates[index] * total)
        total = parts[0][2].scatter(first)
        shares = [shares[0] - rates[0] * total] + moved
        pieces = []
        for share, (_, _, way) in zip(shares, parts):
            pieces.append(way.gather(share))
    return (jnp.concatenate(pieces, 0), influence)


def solution(mesh):
    return jax.shard_map(
        shards,
        mesh=mesh,
        in_specs=(P("row", "basis"), P("row"), P("row", None), P("basis", None), P()),
        out_specs=(P("basis", None), P("row", None)),
        check_vma=False,
    )
```

time: 969 us -> 791 us (0.82)
  waiting for transfers between devices: 706 us -> 426 us
  matrix products: 222 us -> 0 us
  Pallas kernels: 0 us -> 150 us
  starting transfers between devices: 1.88 us -> 148 us
  other arithmetic: 7.73 us -> 27.8 us
  local copies, waits for them, and re-layouts: 7.27 us -> 22.4 us
    all_gather x3, waiting for transfers between devices: 256 us -> 0.06 us  [gather(): return lax.all_gather(own, 'row', axis=0, tiled=True)]
    ppermute x0 -> x65, waiting for transfers between devices: none -> 238 us  [the longest x24 115 us: gather_stage(): arrived = [lax.ppermute(own, 'row', perm_of(k)) for k in range(1, size)]]
    dot_general x7 -> x0, matrix products: 222 us -> none  [the longest x4 115 us: transposed(): lax.dot_general(left, right, (((0,), (0,)), ((), ())), precision=HIGH, pr...]
    reduce_scatter x4, waiting for transfers between devices: 381 us -> 188 us  [scatter(): return lax.psum_scatter(array, 'row', scatter_dimension=0, tiled=True)]
    pallas_call x0 -> x19, Pallas kernels: none -> 150 us  [the longest x7 59.9 us: predict(): pl.pallas_call(functools.partial(predict_kernel, first, steps, start is n...]
    ppermute x0 -> x65, starting transfers between devices: none -> 148 us  [the longest x24 79.4 us: gather_stage(): arrived = [lax.ppermute(own, 'row', perm_of(k)) for k in range(1, size)]]
    psum x3 -> x0, waiting for transfers between devices: 69 us -> none  [predictions(): return lax.psum(partial_value, 'basis')]
    concatenate x0 -> x7, other arithmetic: none -> 12.9 us  [the longest x6 6.68 us: gather_stage(): jnp.concatenate(line, 0)]
  transfers between devices with their start and end apart: 10 -> 72, of which waited for: 10 -> 41; matrix products, arithmetic and copies ran while one was open for 6% -> 4% of each run, Pallas kernels for 0% -> 12%
where the time goes in v1:
time: 791 us; the launch traced here: 790 us
  waiting for transfers between devices  426 us (54%)
  Pallas kernels  150 us (19%)
  starting transfers between devices  148 us (19%)
  other arithmetic  27.8 us (4%)
  local copies, waits for them, and re-layouts  22.4 us (3%)
  between operations  15.4 us (2%)
    reduce_scatter x4, waiting for transfers between devices, scatter(): return lax.psum_scatter(array, 'row', scatter_dimension=0, tiled=True)  188 us
    ppermute x24, waiting for transfers between devices, gather_stage(): arrived = [lax.ppermute(own, 'row', perm_of(k)) for k in range(1, size)]  115 us
    ppermute x32, waiting for transfers between devices, scatter_stage(): lax.ppermute(piece(array, (place + k) % size, rows), 'row', perm_of(k))  95.7 us
    ppermute x24, starting transfers between devices, gather_stage(): arrived = [lax.ppermute(own, 'row', perm_of(k)) for k in range(1, size)]  79.4 us
    ppermute x32, starting transfers between devices, scatter_stage(): lax.ppermute(piece(array, (place + k) % size, rows), 'row', perm_of(k))  61.7 us
    pallas_call x7, Pallas kernels, predict(): pl.pallas_call(functools.partial(predict_kernel, first, steps, start is n...  59.9 us
    pallas_call x3, Pallas kernels, gradient_start(): pl.pallas_call(functools.partial(start_kernel, first, steps), grid=(steps...  38 us
    pallas_call x6, Pallas kernels, gradient_more(): pl.pallas_call(functools.partial(more_kernel, first, steps), grid=(steps,...  32.2 us
  transfers between devices with their start and end apart: 72, of which 41 were waited for; matrix products, arithmetic and copies ran while one was open for 4% of the time, Pallas kernels for 12%

profile of v1, /device:TPU:0, one launch (start us, length us, event | category | flops | bytes accessed | tf_op | source)
XLA Modules:
  0.0 790.3 jit_solution(17982111160324074859)
XLA Ops:
  8.2 9.9 %squares.3.after = f32[5632,128]{1,0:T(8,128)} custom-call(s32[960,128]{1,0:T(8,128)S(1)} %copy-done, f32[960,10240]{1,0:T(8,128)} %design.37, s32[960,128]{1,0:T(8,128)S(1)} %copy-done), custom_call_target="tpu_custom_call" | custom-call | flops 5536481280 | bytes 25001984 | tf_op jit(solution)/shard_map/squares/pallas_call | solution.py:208
  19.2 4.6 squares.4.after
  23.9 5.5 squares.5.extra
  29.4 18.2 %predict.7 = f32[960,128]{1,0:T(8,128)S(1)} custom-call(f32[10240,128]{1,0:T(8,128)S(1)} %bitcast.2, f32[960,10240]{1,0:T(8,128)} %design.37, f32[2560,128]{1,0:T(8,128)S(1)} %squares.5.extra), custom_call_target="tpu_custom_call" | custom-call | flops 10066329600 | bytes 45056000 | tf_op jit(solution)/shard_map/predict/pallas_call | solution.py:101
  49.4 2.9 collective-permute-start.1
  52.3 6.3 collective-permute-done.1
  60.2 12.7 %gradient_start.3 = (f32[5632,128]{1,0:T(8,128)S(1)}, f32[960,128]{1,0:T(8,128)}, bf16[256,1920]{1,0:T(8,128)(2,1)S(1)}) custom-call(f32[960,128]{1,0:T(8,128)S(1)} %maximum_select_fusion.predicted, f32[960,1]{1,0:T(8,128)S(1)} %copy.7.targets, s32[960,128]{1,0:T(8,128)S(1)} %copy-done.1, f32[960,10240]{1,0:T(8,128)} %design.37), custom_call_target="tpu_custom_call" | custom-call | flops 5536481280 | bytes 25001984 | tf_op jit(solution)/shard_map/gradient_start/pallas_call | solution.py:152
  80.4 14.3 %collective-permute-done.3 = f32[1024,128]{1,0:T(8,128)S(1)} collective-permute-done((f32[1024,128]{1,0:T(8,128)}, f32[1024,128]{1,0:T(8,128)S(1)}, u32[]{:S(2)}, u32[]{:S(2)}) %collective-permute-start.3) | collective-permute-done | bytes 524320 | tf_op jit(solution)/shard_map/ppermute | solution.py:247
  94.9 5.1 gradient_more.6
  106.7 5.7 gradient_more.7
  113.5 10.2 %collective-permute-done.7 = f32[1024,128]{1,0:T(8,128)S(1)} collective-permute-done((f32[1024,128]{1,0:T(8,128)S(1)}, f32[1024,128]{1,0:T(8,128)S(1)}, u32[]{:S(2)}, u32[]{:S(2)}) %collective-permute-start.7) | collective-permute-done | bytes 524320 | tf_op jit(solution)/shard_map/ppermute | solution.py:247
  125.6 58.1 %reduce-scatter.7.cloned.1.call-done = f32[704,128]{1,0:T(8,128)} async-done(((f32[5632,128]{1,0:T(8,128)}), f32[704,128]{1,0:T(8,128)}) %reduce-scatter.7.cloned.1.call-update) | async-done | bytes 360464 | tf_op jit(solution)/shard_map/reduce_scatter | solution.py:294
  190.9 2.6 collective-permute-start.16
  193.6 8.1 %collective-permute-start.17 = (f32[320,128]{1,0:T(8,128)S(1)}, f32[320,128]{1,0:T(8,128)S(1)}, u32[]{:S(2)}, u32[]{:S(2)}) collective-permute-start(f32[320,128]{1,0:T(8,128)S(1)} %get-tuple-element.28), channel_id=1, source_target_pairs={{0,16},{4,20},{8,24},{12,28},{16,0},{20,4},{24,8},{28,12},{1,17},{... | collective-permute-start | bytes 491528 | tf_op jit(solution)/shard_map/ppermute | solution.py:247
  201.7 6.3 collective-permute-start.18
  208.1 8.9 %collective-permute-done.9 = f32[256,128]{1,0:T(8,128)S(1)} collective-permute-done((f32[256,128]{1,0:T(8,128)}, f32[256,128]{1,0:T(8,128)S(1)}, u32[]{:S(2)}, u32[]{:S(2)}) %collective-permute-start.9) | collective-permute-done | bytes 131104 | tf_op jit(solution)/shard_map/ppermute | solution.py:247
  220.1 5.9 collective-permute-done.11
  226.0 9.6 %collective-permute-start.13 = (f32[256,128]{1,0:T(8,128)S(1)}, f32[256,128]{1,0:T(8,128)S(1)}, u32[]{:S(2)}, u32[]{:S(2)}) collective-permute-start(f32[256,128]{1,0:T(8,128)S(1)} %get-tuple-element.16), channel_id=1, source_target_pairs={{0,8},{4,12},{8,16},{12,20},{16,24},{20,28},{24,0},{28,4},{1,9},{5... | collective-permute-start | bytes 393224 | tf_op jit(solution)/shard_map/ppermute | solution.py:257
  237.0 5.3 collective-permute-done.13
  242.3 5.3 collective-permute-start.21
  249.4 13.1 %collective-permute-done.21 = f32[320,128]{1,0:T(8,128)S(1)} collective-permute-done((f32[320,128]{1,0:T(8,128)S(1)}, f32[320,128]{1,0:T(8,128)S(1)}, u32[]{:S(2)}, u32[]{:S(2)}) %collective-permute-start.21) | collective-permute-done | bytes 163872 | tf_op jit(solution)/shard_map/ppermute | solution.py:247
  263.2 16.9 %collective-permute-start.23 = (f32[320,128]{1,0:T(8,128)S(1)}, f32[320,128]{1,0:T(8,128)S(1)}, u32[]{:S(2)}, u32[]{:S(2)}) collective-permute-start(f32[320,128]{1,0:T(8,128)S(1)} %get-tuple-element.18), channel_id=1, source_target_pairs={{0,24},{4,28},{8,0},{12,4},{16,8},{20,12},{24,16},{28,20},{1,25},{... | collective-permute-start | bytes 491528 | tf_op jit(solution)/shard_map/ppermute | solution.py:257
  283.0 3.9 collective-permute-done.24
  290.3 4.4 collective-permute-done.14
  296.3 7.2 collective-permute-done.26
  304.6 5.6 predict.8.extra
  310.3 4.8 predict.9.extra
  316.9 10.4 %predict.10 = f32[960,128]{1,0:T(8,128)S(1)} custom-call(f32[5632,128]{1,0:T(8,128)S(1)} %copy-done.16, f32[960,10240]{1,0:T(8,128)} %design.37, f32[960,128]{1,0:T(8,128)S(1)} %predict.9.extra), custom_call_target="tpu_custom_call" | custom-call | flops 5536481280 | bytes 25001984 | tf_op jit(solution)/shard_map/predict/pallas_call | solution.py:101
  330.5 6.6 collective-permute-done.28
  338.8 12.7 %gradient_start.4 = (f32[5632,128]{1,0:T(8,128)S(1)}, f32[960,128]{1,0:T(8,128)}, bf16[256,1920]{1,0:T(8,128)(2,1)S(1)}) custom-call(f32[960,128]{1,0:T(8,128)S(1)} %maximum_select_fusion.1.predicted, f32[960,1]{1,0:T(8,128)S(1)} %copy-done.6, s32[960,128]{1,0:T(8,128)S(1)} %copy-done.1, f32[960,10240]{1,0:T(8,128)} %design.37), custom_call_target="tpu_custom_call" | custom-call | flops 5536481280 | bytes 25001984 | tf_op jit(solution)/shard_map/gradient_start/pallas_call | solution.py:152
  354.0 4.9 gradient_more.8
  361.2 5.7 gradient_more.9
  368.4 63.6 %reduce-scatter.9.cloned.1.call-done = f32[704,128]{1,0:T(8,128)} async-done(((f32[5632,128]{1,0:T(8,128)}), f32[704,128]{1,0:T(8,128)}) %reduce-scatter.9.cloned.1.call-update) | async-done | bytes 360464 | tf_op jit(solution)/shard_map/reduce_scatter | solution.py:294
  439.9 3.7 collective-permute-done.31
  443.6 6.9 collective-permute-done.32
  450.6 10.1 %collective-permute-start.34 = (f32[256,128]{1,0:T(8,128)S(1)}, f32[256,128]{1,0:T(8,128)S(1)}, u32[]{:S(2)}, u32[]{:S(2)}) collective-permute-start(f32[256,128]{1,0:T(8,128)S(1)} %multiply_subtract_fusion.7), channel_id=1, source_target_pairs={{0,24},{4,28},{8,0},{12,4},{16,8},{20,12},{24,16},{28,20},{1,25},{... | collective-permute-start | bytes 393224 | tf_op jit(solution)/shard_map/ppermute | solution.py:257
  462.5 2.9 collective-permute-start.39
  466.3 2.5 collective-permute-start.41
  468.8 20.0 %collective-permute-done.35 = f32[256,128]{1,0:T(8,128)S(1)} collective-permute-done((f32[256,128]{1,0:T(8,128)S(1)}, f32[256,128]{1,0:T(8,128)S(1)}, u32[]{:S(2)}, u32[]{:S(2)}) %collective-permute-start.35) | collective-permute-done | bytes 131104 | tf_op jit(solution)/shard_map/ppermute | solution.py:257
  488.9 11.7 %collective-permute-done.40 = f32[320,128]{1,0:T(8,128)S(1)} collective-permute-done((f32[320,128]{1,0:T(8,128)S(1)}, f32[320,128]{1,0:T(8,128)S(1)}, u32[]{:S(2)}, u32[]{:S(2)}) %collective-permute-start.40) | collective-permute-done | bytes 163872 | tf_op jit(solution)/shard_map/ppermute | solution.py:247
  500.7 7.8 collective-permute-start.42
  508.5 2.7 collective-permute-start.43
  513.1 10.9 %collective-permute-done.43 = f32[320,128]{1,0:T(8,128)S(1)} collective-permute-done((f32[320,128]{1,0:T(8,128)S(1)}, f32[320,128]{1,0:T(8,128)S(1)}, u32[]{:S(2)}, u32[]{:S(2)}) %collective-permute-start.43) | collective-permute-done | bytes 163872 | tf_op jit(solution)/shard_map/ppermute | solution.py:257
  526.5 13.0 %collective-permute-done.45 = f32[1280,128]{1,0:T(8,128)S(1)} collective-permute-done((f32[1280,128]{1,0:T(8,128)S(1)}, f32[1280,128]{1,0:T(8,128)S(1)}, u32[]{:S(2)}, u32[]{:S(2)}) %collective-permute-start.45) | collective-permute-done | bytes 655392 | tf_op jit(solution)/shard_map/ppermute | solution.py:257
  540.7 5.6 predict.11.extra
  546.3 4.8 predict.12.extra
  553.0 10.4 %predict.13 = f32[960,128]{1,0:T(8,128)S(1)} custom-call(f32[5632,128]{1,0:T(8,128)S(1)} %copy-done.17, f32[960,10240]{1,0:T(8,128)} %design.37, f32[960,128]{1,0:T(8,128)S(1)} %predict.12.extra), custom_call_target="tpu_custom_call" | custom-call | flops 5536481280 | bytes 25001984 | tf_op jit(solution)/shard_map/predict/pallas_call | solution.py:101
  566.4 6.7 collective-permute-done.47
  574.8 12.7 %gradient_start.5 = (f32[5632,128]{1,0:T(8,128)S(1)}, f32[960,128]{1,0:T(8,128)}, bf16[256,1920]{1,0:T(8,128)(2,1)S(1)}) custom-call(f32[960,128]{1,0:T(8,128)S(1)} %maximum_select_fusion.2.predicted, f32[960,1]{1,0:T(8,128)S(1)} %copy-done.6, s32[960,128]{1,0:T(8,128)S(1)} %copy-done.1, f32[960,10240]{1,0:T(8,128)} %design.37), custom_call_target="tpu_custom_call" | custom-call | flops 5536481280 | bytes 25001984 | tf_op jit(solution)/shard_map/gradient_start/pallas_call | solution.py:152
  589.1 5.0 gradient_more.10
  596.2 66.2 %reduce-scatter.11.cloned.1.call-done = f32[704,128]{1,0:T(8,128)} async-done(((f32[5632,128]{1,0:T(8,128)}), f32[704,128]{1,0:T(8,128)}) %reduce-scatter.11.cloned.1.call-update) | async-done | bytes 360464 | tf_op jit(solution)/shard_map/reduce_scatter | solution.py:294
  664.2 5.8 gradient_more.11
  677.3 5.9 collective-permute-done.50
  683.3 8.2 %collective-permute-done.51 = f32[256,128]{1,0:T(8,128)S(1)} collective-permute-done((f32[256,128]{1,0:T(8,128)S(1)}, f32[256,128]{1,0:T(8,128)S(1)}, u32[]{:S(2)}, u32[]{:S(2)}) %collective-permute-start.51) | collective-permute-done | bytes 131104 | tf_op jit(solution)/shard_map/ppermute | solution.py:247
  691.5 9.2 %collective-permute-start.53 = (f32[256,128]{1,0:T(8,128)S(1)}, f32[256,128]{1,0:T(8,128)S(1)}, u32[]{:S(2)}, u32[]{:S(2)}) collective-permute-start(f32[256,128]{1,0:T(8,128)S(1)} %multiply_subtract_fusion.6), channel_id=1, source_target_pairs={{0,24},{4,28},{8,0},{12,4},{16,8},{20,12},{24,16},{28,20},{1,25},{... | collective-permute-start | bytes 393224 | tf_op jit(solution)/shard_map/ppermute | solution.py:257
  701.5 2.9 collective-permute-start.58
  707.1 3.2 collective-permute-start.60
  710.3 18.4 %collective-permute-done.54 = f32[256,128]{1,0:T(8,128)S(1)} collective-permute-done((f32[256,128]{1,0:T(8,128)S(1)}, f32[256,128]{1,0:T(8,128)S(1)}, u32[]{:S(2)}, u32[]{:S(2)}) %collective-permute-start.54) | collective-permute-done | bytes 131104 | tf_op jit(solution)/shard_map/ppermute | solution.py:257
  728.8 10.9 %collective-permute-done.59 = f32[320,128]{1,0:T(8,128)S(1)} collective-permute-done((f32[320,128]{1,0:T(8,128)S(1)}, f32[320,128]{1,0:T(8,128)S(1)}, u32[]{:S(2)}, u32[]{:S(2)}) %collective-permute-start.59) | collective-permute-done | bytes 163872 | tf_op jit(solution)/shard_map/ppermute | solution.py:247
  739.8 12.6 %collective-permute-start.61 = (f32[320,128]{1,0:T(8,128)S(1)}, f32[320,128]{1,0:T(8,128)S(1)}, u32[]{:S(2)}, u32[]{:S(2)}) collective-permute-start(f32[320,128]{1,0:T(8,128)S(1)} %multiply_subtract_fusion.3), channel_id=1, source_target_pairs={{0,24},{4,28},{8,0},{12,4},{16,8},{20,12},{24,16},{28,20},{1,25},{... | collective-permute-start | bytes 491528 | tf_op jit(solution)/shard_map/ppermute | solution.py:257
  755.4 5.9 collective-permute-done.62
  762.4 5.3 collective-permute-done.56
  768.6 7.4 collective-permute-done.64
  777.2 6.3 pad_maximum_fusion
  (276 shorter events, 104.0 us)
Async XLA Ops:
  7.2 118.4 %reduce-scatter.5.cloned.1.call-start = ((), (), s32[]{:S(2)}) async-start(), calls=%async_computation.4 | async-start | bytes 3244032 | tf_op jit(solution)/shard_map/reduce_scatter | solution.py:294
  18.2 165.5 %reduce-scatter.7.cloned.1.call-start = ((), (), s32[]{:S(2)}) async-start(), calls=%async_computation.5 | async-start | bytes 3244032 | tf_op jit(solution)/shard_map/reduce_scatter | solution.py:294
  49.4 9.2 %collective-permute-start.1 = (f32[480,128]{1,0:T(8,128)S(1)}, f32[480,128]{1,0:T(8,128)S(1)}, u32[]{:S(2)}, u32[]{:S(2)}) collective-permute-start(f32[480,128]{1,0:T(8,128)S(1)} %dynamic-slice_add_fusion.10), channel_id=1, source_target_pairs={{0,2},{1,3},{2,0},{3,1},{4,6},{5,7},{6,4},{7,5},{8,10},{9,11},{10,... | collective-permute-start | bytes 737288 | tf_op jit(solution)/shard_map/ppermute | solution.py:311
  75.4 239.7 %all-gather.4.cloned.1.call-start = ((), (), s32[]{:S(2)}) async-start(), calls=%async_computation.6 | async-start | bytes 3244032 | tf_op jit(solution)/shard_map/all_gather | solution.py:297
  77.5 17.3 %collective-permute-start.3 = (f32[1024,128]{1,0:T(8,128)}, f32[1024,128]{1,0:T(8,128)S(1)}, u32[]{:S(2)}, u32[]{:S(2)}) collective-permute-start(f32[1024,128]{1,0:T(8,128)} %constant_dynamic-slice_fusion.38), channel_id=1, source_target_pairs={{0,4},{4,0},{8,12},{12,8},{16,20},{20,16},{24,28},{28,24},{1,5},{5... | collective-permute-start | bytes 1572872 | tf_op jit(solution)/shard_map/ppermute | solution.py:247
  80.2 105.5 %collective-permute-start.15 = (f32[1280,128]{1,0:T(8,128)}, f32[1280,128]{1,0:T(8,128)}, u32[]{:S(2)}, u32[]{:S(2)}) collective-permute-start(f32[1280,128]{1,0:T(8,128)} %constant_dynamic-slice_fusion.29), channel_id=1, source_target_pairs={{0,4},{4,0},{8,12},{12,8},{16,20},{20,16},{24,28},{28,24},{1,5},{5... | collective-permute-start | bytes 1966088 | tf_op jit(solution)/shard_map/ppermute | solution.py:247
  100.0 23.6 %collective-permute-start.7 = (f32[1024,128]{1,0:T(8,128)S(1)}, f32[1024,128]{1,0:T(8,128)S(1)}, u32[]{:S(2)}, u32[]{:S(2)}) collective-permute-start(f32[1024,128]{1,0:T(8,128)S(1)} %constant_dynamic-slice_fusion.34), channel_id=1, source_target_pairs={{0,4},{4,0},{8,12},{12,8},{16,20},{20,16},{24,28},{28,24},{1,5},{5... | collective-permute-start | bytes 1572872 | tf_op jit(solution)/shard_map/ppermute | solution.py:247
  101.2 86.4 %collective-permute-start.4 = (f32[256,128]{1,0:T(8,128)}, f32[256,128]{1,0:T(8,128)S(1)}, u32[]{:S(2)}, u32[]{:S(2)}) collective-permute-start(f32[256,128]{1,0:T(8,128)} %get-tuple-element.38), channel_id=1, source_target_pairs={{0,8},{4,12},{8,16},{12,20},{16,24},{20,28},{24,0},{28,4},{1,9},{5... | collective-permute-start | bytes 393224 | tf_op jit(solution)/shard_map/ppermute | solution.py:247
  102.9 84.9 %collective-permute-start.5 = (f32[256,128]{1,0:T(8,128)}, f32[256,128]{1,0:T(8,128)}, u32[]{:S(2)}, u32[]{:S(2)}) collective-permute-start(f32[256,128]{1,0:T(8,128)} %get-tuple-element.40), channel_id=1, source_target_pairs={{0,16},{4,20},{8,24},{12,28},{16,0},{20,4},{24,8},{28,12},{1,17},{... | collective-permute-start | bytes 393224 | tf_op jit(solution)/shard_map/ppermute | solution.py:247
  105.3 85.6 %collective-permute-start.6 = (f32[256,128]{1,0:T(8,128)}, f32[256,128]{1,0:T(8,128)}, u32[]{:S(2)}, u32[]{:S(2)}) collective-permute-start(f32[256,128]{1,0:T(8,128)} %get-tuple-element.39), channel_id=1, source_target_pairs={{0,24},{4,28},{8,0},{12,4},{16,8},{20,12},{24,16},{28,20},{1,25},{... | collective-permute-start | bytes 393224 | tf_op jit(solution)/shard_map/ppermute | solution.py:247
  123.6 95.2 %collective-permute-start.19 = (f32[1280,128]{1,0:T(8,128)}, f32[1280,128]{1,0:T(8,128)}, u32[]{:S(2)}, u32[]{:S(2)}) collective-permute-start(f32[1280,128]{1,0:T(8,128)} %constant_dynamic-slice_fusion.25), channel_id=1, source_target_pairs={{0,4},{4,0},{8,12},{12,8},{16,20},{20,16},{24,28},{28,24},{1,5},{5... | collective-permute-start | bytes 1966088 | tf_op jit(solution)/shard_map/ppermute | solution.py:247
  185.6 246.4 %reduce-scatter.9.cloned.1.call-start = ((), (), s32[]{:S(2)}) async-start(), calls=%async_computation.7 | async-start | bytes 3244032 | tf_op jit(solution)/shard_map/reduce_scatter | solution.py:294
  185.7 8.0 %collective-permute-start.10 = (f32[256,128]{1,0:T(8,128)}, f32[256,128]{1,0:T(8,128)S(1)}, u32[]{:S(2)}, u32[]{:S(2)}) collective-permute-start(f32[256,128]{1,0:T(8,128)} %get-tuple-element.42), channel_id=1, source_target_pairs={{0,24},{4,28},{8,0},{12,4},{16,8},{20,12},{24,16},{28,20},{1,25},{... | collective-permute-start | bytes 393224 | tf_op jit(solution)/shard_map/ppermute | solution.py:247
  187.6 14.2 %collective-permute-start.8 = (f32[256,128]{1,0:T(8,128)}, f32[256,128]{1,0:T(8,128)S(1)}, u32[]{:S(2)}, u32[]{:S(2)}) collective-permute-start(f32[256,128]{1,0:T(8,128)} %get-tuple-element.41), channel_id=1, source_target_pairs={{0,8},{4,12},{8,16},{12,20},{16,24},{20,28},{24,0},{28,4},{1,9},{5... | collective-permute-start | bytes 393224 | tf_op jit(solution)/shard_map/ppermute | solution.py:247
  187.8 29.2 %collective-permute-start.9 = (f32[256,128]{1,0:T(8,128)}, f32[256,128]{1,0:T(8,128)S(1)}, u32[]{:S(2)}, u32[]{:S(2)}) collective-permute-start(f32[256,128]{1,0:T(8,128)} %get-tuple-element.43), channel_id=1, source_target_pairs={{0,16},{4,20},{8,24},{12,28},{16,0},{20,4},{24,8},{28,12},{1,17},{... | collective-permute-start | bytes 393224 | tf_op jit(solution)/shard_map/ppermute | solution.py:247
  190.9 56.7 %collective-permute-start.16 = (f32[320,128]{1,0:T(8,128)S(1)}, f32[320,128]{1,0:T(8,128)S(1)}, u32[]{:S(2)}, u32[]{:S(2)}) collective-permute-start(f32[320,128]{1,0:T(8,128)S(1)} %get-tuple-element.26), channel_id=1, source_target_pairs={{0,8},{4,12},{8,16},{12,20},{16,24},{20,28},{24,0},{28,4},{1,9},{5... | collective-permute-start | bytes 491528 | tf_op jit(solution)/shard_map/ppermute | solution.py:247
  193.6 54.1 %collective-permute-start.17 = (f32[320,128]{1,0:T(8,128)S(1)}, f32[320,128]{1,0:T(8,128)S(1)}, u32[]{:S(2)}, u32[]{:S(2)}) collective-permute-start(f32[320,128]{1,0:T(8,128)S(1)} %get-tuple-element.28), channel_id=1, source_target_pairs={{0,16},{4,20},{8,24},{12,28},{16,0},{20,4},{24,8},{28,12},{1,17},{... | collective-permute-start | bytes 491528 | tf_op jit(solution)/shard_map/ppermute | solution.py:247
  201.7 46.0 %collective-permute-start.18 = (f32[320,128]{1,0:T(8,128)S(1)}, f32[320,128]{1,0:T(8,128)S(1)}, u32[]{:S(2)}, u32[]{:S(2)}) collective-permute-start(f32[320,128]{1,0:T(8,128)S(1)} %get-tuple-element.27), channel_id=1, source_target_pairs={{0,24},{4,28},{8,0},{12,4},{16,8},{20,12},{24,16},{28,20},{1,25},{... | collective-permute-start | bytes 491528 | tf_op jit(solution)/shard_map/ppermute | solution.py:247
  218.8 7.2 collective-permute-start.11
  218.8 18.2 %collective-permute-start.12 = (f32[256,128]{1,0:T(8,128)S(1)}, f32[256,128]{1,0:T(8,128)S(1)}, u32[]{:S(2)}, u32[]{:S(2)}) collective-permute-start(f32[256,128]{1,0:T(8,128)S(1)} %get-tuple-element.16), channel_id=1, source_target_pairs={{0,16},{4,20},{8,24},{12,28},{16,0},{20,4},{24,8},{28,12},{1,17},{... | collective-permute-start | bytes 393224 | tf_op jit(solution)/shard_map/ppermute | solution.py:257
  226.0 16.3 %collective-permute-start.13 = (f32[256,128]{1,0:T(8,128)S(1)}, f32[256,128]{1,0:T(8,128)S(1)}, u32[]{:S(2)}, u32[]{:S(2)}) collective-permute-start(f32[256,128]{1,0:T(8,128)S(1)} %get-tuple-element.16), channel_id=1, source_target_pairs={{0,8},{4,12},{8,16},{12,20},{16,24},{20,28},{24,0},{28,4},{1,9},{5... | collective-permute-start | bytes 393224 | tf_op jit(solution)/shard_map/ppermute | solution.py:257
  237.0 12.4 %collective-permute-start.20 = (f32[320,128]{1,0:T(8,128)S(1)}, f32[320,128]{1,0:T(8,128)S(1)}, u32[]{:S(2)}, u32[]{:S(2)}) collective-permute-start(f32[320,128]{1,0:T(8,128)S(1)} %get-tuple-element.29), channel_id=1, source_target_pairs={{0,8},{4,12},{8,16},{12,20},{16,24},{20,28},{24,0},{28,4},{1,9},{5... | collective-permute-start | bytes 491528 | tf_op jit(solution)/shard_map/ppermute | solution.py:247
  242.3 20.2 %collective-permute-start.21 = (f32[320,128]{1,0:T(8,128)S(1)}, f32[320,128]{1,0:T(8,128)S(1)}, u32[]{:S(2)}, u32[]{:S(2)}) collective-permute-start(f32[320,128]{1,0:T(8,128)S(1)} %get-tuple-element.31), channel_id=1, source_target_pairs={{0,16},{4,20},{8,24},{12,28},{16,0},{20,4},{24,8},{28,12},{1,17},{... | collective-permute-start | bytes 491528 | tf_op jit(solution)/shard_map/ppermute | solution.py:247
  247.6 14.8 %collective-permute-start.22 = (f32[320,128]{1,0:T(8,128)S(1)}, f32[320,128]{1,0:T(8,128)S(1)}, u32[]{:S(2)}, u32[]{:S(2)}) collective-permute-start(f32[320,128]{1,0:T(8,128)S(1)} %get-tuple-element.30), channel_id=1, source_target_pairs={{0,24},{4,28},{8,0},{12,4},{16,8},{20,12},{24,16},{28,20},{1,25},{... | collective-permute-start | bytes 491528 | tf_op jit(solution)/shard_map/ppermute | solution.py:247
  263.2 19.8 %collective-permute-start.23 = (f32[320,128]{1,0:T(8,128)S(1)}, f32[320,128]{1,0:T(8,128)S(1)}, u32[]{:S(2)}, u32[]{:S(2)}) collective-permute-start(f32[320,128]{1,0:T(8,128)S(1)} %get-tuple-element.18), channel_id=1, source_target_pairs={{0,24},{4,28},{8,0},{12,4},{16,8},{20,12},{24,16},{28,20},{1,25},{... | collective-permute-start | bytes 491528 | tf_op jit(solution)/shard_map/ppermute | solution.py:257
  280.2 14.4 %collective-permute-start.14 = (f32[1024,128]{1,0:T(8,128)S(1)}, f32[1024,128]{1,0:T(8,128)}, u32[]{:S(2)}, u32[]{:S(2)}) collective-permute-start(f32[1024,128]{1,0:T(8,128)S(1)} %constant_dynamic-slice_fusion.30), channel_id=1, source_target_pairs={{0,4},{4,0},{8,12},{12,8},{16,20},{20,16},{24,28},{28,24},{1,5},{5... | collective-permute-start | bytes 1572872 | tf_op jit(solution)/shard_map/ppermute | solution.py:257
  289.0 14.6 %collective-permute-start.26 = (f32[1280,128]{1,0:T(8,128)S(1)}, f32[1280,128]{1,0:T(8,128)S(1)}, u32[]{:S(2)}, u32[]{:S(2)}) collective-permute-start(f32[1280,128]{1,0:T(8,128)S(1)} %constant_dynamic-slice_fusion.21), channel_id=1, source_target_pairs={{0,4},{4,0},{8,12},{12,8},{16,20},{20,16},{24,28},{28,24},{1,5},{5... | collective-permute-start | bytes 1966088 | tf_op jit(solution)/shard_map/ppermute | solution.py:257
  329.0 8.1 %collective-permute-start.28 = (f32[480,128]{1,0:T(8,128)S(1)}, f32[480,128]{1,0:T(8,128)S(1)}, u32[]{:S(2)}, u32[]{:S(2)}) collective-permute-start(f32[480,128]{1,0:T(8,128)S(1)} %dynamic-slice_add_fusion.9), channel_id=1, source_target_pairs={{0,2},{1,3},{2,0},{3,1},{4,6},{5,7},{6,4},{7,5},{8,10},{9,11},{10,... | collective-permute-start | bytes 737288 | tf_op jit(solution)/shard_map/ppermute | solution.py:311
  353.0 198.1 %all-gather.6.cloned.1.call-start = ((), (), s32[]{:S(2)}) async-start(), calls=%async_computation.8 | async-start | bytes 3244032 | tf_op jit(solution)/shard_map/all_gather | solution.py:297
  359.7 74.4 %collective-permute-start.30 = (f32[1024,128]{1,0:T(8,128)}, f32[1024,128]{1,0:T(8,128)}, u32[]{:S(2)}, u32[]{:S(2)}) collective-permute-start(f32[1024,128]{1,0:T(8,128)} %constant_dynamic-slice_fusion.19), channel_id=1, source_target_pairs={{0,4},{4,0},{8,12},{12,8},{16,20},{20,16},{24,28},{28,24},{1,5},{5... | collective-permute-start | bytes 1572872 | tf_op jit(solution)/shard_map/ppermute | solution.py:247
  367.8 93.5 %collective-permute-start.38 = (f32[1280,128]{1,0:T(8,128)}, f32[1280,128]{1,0:T(8,128)}, u32[]{:S(2)}, u32[]{:S(2)}) collective-permute-start(f32[1280,128]{1,0:T(8,128)} %constant_dynamic-slice_fusion.14), channel_id=1, source_target_pairs={{0,4},{4,0},{8,12},{12,8},{16,20},{20,16},{24,28},{28,24},{1,5},{5... | collective-permute-start | bytes 1966088 | tf_op jit(solution)/shard_map/ppermute | solution.py:247
  434.0 228.4 %reduce-scatter.11.cloned.1.call-start = ((), (), s32[]{:S(2)}) async-start(), calls=%async_computation.9 | async-start | bytes 3244032 | tf_op jit(solution)/shard_map/reduce_scatter | solution.py:294
  435.3 8.3 %collective-permute-start.31 = (f32[256,128]{1,0:T(8,128)S(1)}, f32[256,128]{1,0:T(8,128)S(1)}, u32[]{:S(2)}, u32[]{:S(2)}) collective-permute-start(f32[256,128]{1,0:T(8,128)S(1)} %get-tuple-element.35), channel_id=1, source_target_pairs={{0,8},{4,12},{8,16},{12,20},{16,24},{20,28},{24,0},{28,4},{1,9},{5... | collective-permute-start | bytes 393224 | tf_op jit(solution)/shard_map/ppermute | solution.py:247
  436.4 14.1 %collective-permute-start.32 = (f32[256,128]{1,0:T(8,128)S(1)}, f32[256,128]{1,0:T(8,128)S(1)}, u32[]{:S(2)}, u32[]{:S(2)}) collective-permute-start(f32[256,128]{1,0:T(8,128)S(1)} %get-tuple-element.37), channel_id=1, source_target_pairs={{0,16},{4,20},{8,24},{12,28},{16,0},{20,4},{24,8},{28,12},{1,17},{... | collective-permute-start | bytes 393224 | tf_op jit(solution)/shard_map/ppermute | solution.py:247
  437.8 12.7 %collective-permute-start.33 = (f32[256,128]{1,0:T(8,128)S(1)}, f32[256,128]{1,0:T(8,128)S(1)}, u32[]{:S(2)}, u32[]{:S(2)}) collective-permute-start(f32[256,128]{1,0:T(8,128)S(1)} %get-tuple-element.36), channel_id=1, source_target_pairs={{0,24},{4,28},{8,0},{12,4},{16,8},{20,12},{24,16},{28,20},{1,25},{... | collective-permute-start | bytes 393224 | tf_op jit(solution)/shard_map/ppermute | solution.py:247
  450.6 15.8 %collective-permute-start.34 = (f32[256,128]{1,0:T(8,128)S(1)}, f32[256,128]{1,0:T(8,128)S(1)}, u32[]{:S(2)}, u32[]{:S(2)}) collective-permute-start(f32[256,128]{1,0:T(8,128)S(1)} %multiply_subtract_fusion.7), channel_id=1, source_target_pairs={{0,24},{4,28},{8,0},{12,4},{16,8},{20,12},{24,16},{28,20},{1,25},{... | collective-permute-start | bytes 393224 | tf_op jit(solution)/shard_map/ppermute | solution.py:257
  460.7 28.2 %collective-permute-start.35 = (f32[256,128]{1,0:T(8,128)S(1)}, f32[256,128]{1,0:T(8,128)S(1)}, u32[]{:S(2)}, u32[]{:S(2)}) collective-permute-start(f32[256,128]{1,0:T(8,128)S(1)} %multiply_subtract_fusion.7), channel_id=1, source_target_pairs={{0,16},{4,20},{8,24},{12,28},{16,0},{20,4},{24,8},{28,12},{1,17},{... | collective-permute-start | bytes 393224 | tf_op jit(solution)/shard_map/ppermute | solution.py:257
  460.7 28.2 %collective-permute-start.36 = (f32[256,128]{1,0:T(8,128)S(1)}, f32[256,128]{1,0:T(8,128)S(1)}, u32[]{:S(2)}, u32[]{:S(2)}) collective-permute-start(f32[256,128]{1,0:T(8,128)S(1)} %multiply_subtract_fusion.7), channel_id=1, source_target_pairs={{0,8},{4,12},{8,16},{12,20},{16,24},{20,28},{24,0},{28,4},{1,9},{5... | collective-permute-start | bytes 393224 | tf_op jit(solution)/shard_map/ppermute | solution.py:257
  462.5 26.4 %collective-permute-start.39 = (f32[320,128]{1,0:T(8,128)S(1)}, f32[320,128]{1,0:T(8,128)S(1)}, u32[]{:S(2)}, u32[]{:S(2)}) collective-permute-start(f32[320,128]{1,0:T(8,128)S(1)} %get-tuple-element.23), channel_id=1, source_target_pairs={{0,8},{4,12},{8,16},{12,20},{16,24},{20,28},{24,0},{28,4},{1,9},{5... | collective-permute-start | bytes 491528 | tf_op jit(solution)/shard_map/ppermute | solution.py:247
  465.4 35.2 %collective-permute-start.40 = (f32[320,128]{1,0:T(8,128)S(1)}, f32[320,128]{1,0:T(8,128)S(1)}, u32[]{:S(2)}, u32[]{:S(2)}) collective-permute-start(f32[320,128]{1,0:T(8,128)S(1)} %get-tuple-element.25), channel_id=1, source_target_pairs={{0,16},{4,20},{8,24},{12,28},{16,0},{20,4},{24,8},{28,12},{1,17},{... | collective-permute-start | bytes 491528 | tf_op jit(solution)/shard_map/ppermute | solution.py:247
  466.3 34.3 %collective-permute-start.41 = (f32[320,128]{1,0:T(8,128)S(1)}, f32[320,128]{1,0:T(8,128)S(1)}, u32[]{:S(2)}, u32[]{:S(2)}) collective-permute-start(f32[320,128]{1,0:T(8,128)S(1)} %get-tuple-element.24), channel_id=1, source_target_pairs={{0,24},{4,28},{8,0},{12,4},{16,8},{20,12},{24,16},{28,20},{1,25},{... | collective-permute-start | bytes 491528 | tf_op jit(solution)/shard_map/ppermute | solution.py:247
  500.7 12.4 %collective-permute-start.42 = (f32[320,128]{1,0:T(8,128)S(1)}, f32[320,128]{1,0:T(8,128)S(1)}, u32[]{:S(2)}, u32[]{:S(2)}) collective-permute-start(f32[320,128]{1,0:T(8,128)S(1)} %multiply_subtract_fusion.4), channel_id=1, source_target_pairs={{0,24},{4,28},{8,0},{12,4},{16,8},{20,12},{24,16},{28,20},{1,25},{... | collective-permute-start | bytes 491528 | tf_op jit(solution)/shard_map/ppermute | solution.py:257
  508.5 15.5 %collective-permute-start.43 = (f32[320,128]{1,0:T(8,128)S(1)}, f32[320,128]{1,0:T(8,128)S(1)}, u32[]{:S(2)}, u32[]{:S(2)}) collective-permute-start(f32[320,128]{1,0:T(8,128)S(1)} %multiply_subtract_fusion.4), channel_id=1, source_target_pairs={{0,16},{4,20},{8,24},{12,28},{16,0},{20,4},{24,8},{28,12},{1,17},{... | collective-permute-start | bytes 491528 | tf_op jit(solution)/shard_map/ppermute | solution.py:257
  511.2 14.4 %collective-permute-start.37 = (f32[1024,128]{1,0:T(8,128)S(1)}, f32[1024,128]{1,0:T(8,128)S(1)}, u32[]{:S(2)}, u32[]{:S(2)}) collective-permute-start(f32[1024,128]{1,0:T(8,128)S(1)} %constant_dynamic-slice_fusion.15), channel_id=1, source_target_pairs={{0,4},{4,0},{8,12},{12,8},{16,20},{20,16},{24,28},{28,24},{1,5},{5... | collective-permute-start | bytes 1572872 | tf_op jit(solution)/shard_map/ppermute | solution.py:257
  513.1 11.0 %collective-permute-start.44 = (f32[320,128]{1,0:T(8,128)S(1)}, f32[320,128]{1,0:T(8,128)S(1)}, u32[]{:S(2)}, u32[]{:S(2)}) collective-permute-start(f32[320,128]{1,0:T(8,128)S(1)} %multiply_subtract_fusion.4), channel_id=1, source_target_pairs={{0,8},{4,12},{8,16},{12,20},{16,24},{20,28},{24,0},{28,4},{1,9},{5... | collective-permute-start | bytes 491528 | tf_op jit(solution)/shard_map/ppermute | solution.py:257
  524.2 15.3 %collective-permute-start.45 = (f32[1280,128]{1,0:T(8,128)S(1)}, f32[1280,128]{1,0:T(8,128)S(1)}, u32[]{:S(2)}, u32[]{:S(2)}) collective-permute-start(f32[1280,128]{1,0:T(8,128)S(1)} %constant_dynamic-slice_fusion.10), channel_id=1, source_target_pairs={{0,4},{4,0},{8,12},{12,8},{16,20},{20,16},{24,28},{28,24},{1,5},{5... | collective-permute-start | bytes 1966088 | tf_op jit(solution)/shard_map/ppermute | solution.py:257
  565.1 8.1 %collective-permute-start.47 = (f32[480,128]{1,0:T(8,128)S(1)}, f32[480,128]{1,0:T(8,128)S(1)}, u32[]{:S(2)}, u32[]{:S(2)}) collective-permute-start(f32[480,128]{1,0:T(8,128)S(1)} %dynamic-slice_add_fusion.8), channel_id=1, source_target_pairs={{0,2},{1,3},{2,0},{3,1},{4,6},{5,7},{6,4},{7,5},{8,10},{9,11},{10,... | collective-permute-start | bytes 737288 | tf_op jit(solution)/shard_map/ppermute | solution.py:311
  589.0 188.2 %all-gather.8.cloned.1.call-start = ((), (), s32[]{:S(2)}) async-start(), calls=%async_computation.10 | async-start | bytes 3244032 | tf_op jit(solution)/shard_map/all_gather | solution.py:297
  594.9 76.4 %collective-permute-start.49 = (f32[1024,128]{1,0:T(8,128)}, f32[1024,128]{1,0:T(8,128)}, u32[]{:S(2)}, u32[]{:S(2)}) collective-permute-start(f32[1024,128]{1,0:T(8,128)} %constant_dynamic-slice_fusion.8), channel_id=1, source_target_pairs={{0,4},{4,0},{8,12},{12,8},{16,20},{20,16},{24,28},{28,24},{1,5},{5... | collective-permute-start | bytes 1572872 | tf_op jit(solution)/shard_map/ppermute | solution.py:247
  670.1 31.3 %collective-permute-start.57 = (f32[1280,128]{1,0:T(8,128)S(1)}, f32[1280,128]{1,0:T(8,128)S(1)}, u32[]{:S(2)}, u32[]{:S(2)}) collective-permute-start(f32[1280,128]{1,0:T(8,128)S(1)} %constant_dynamic-slice_fusion.3), channel_id=1, source_target_pairs={{0,4},{4,0},{8,12},{12,8},{16,20},{20,16},{24,28},{28,24},{1,5},{5... | collective-permute-start | bytes 1966088 | tf_op jit(solution)/shard_map/ppermute | solution.py:247
  672.5 10.7 %collective-permute-start.50 = (f32[256,128]{1,0:T(8,128)S(1)}, f32[256,128]{1,0:T(8,128)S(1)}, u32[]{:S(2)}, u32[]{:S(2)}) collective-permute-start(f32[256,128]{1,0:T(8,128)S(1)} %get-tuple-element.32), channel_id=1, source_target_pairs={{0,8},{4,12},{8,16},{12,20},{16,24},{20,28},{24,0},{28,4},{1,9},{5... | collective-permute-start | bytes 393224 | tf_op jit(solution)/shard_map/ppermute | solution.py:247
  673.9 17.5 %collective-permute-start.51 = (f32[256,128]{1,0:T(8,128)S(1)}, f32[256,128]{1,0:T(8,128)S(1)}, u32[]{:S(2)}, u32[]{:S(2)}) collective-permute-start(f32[256,128]{1,0:T(8,128)S(1)} %get-tuple-element.34), channel_id=1, source_target_pairs={{0,16},{4,20},{8,24},{12,28},{16,0},{20,4},{24,8},{28,12},{1,17},{... | collective-permute-start | bytes 393224 | tf_op jit(solution)/shard_map/ppermute | solution.py:247
  675.0 16.4 %collective-permute-start.52 = (f32[256,128]{1,0:T(8,128)S(1)}, f32[256,128]{1,0:T(8,128)S(1)}, u32[]{:S(2)}, u32[]{:S(2)}) collective-permute-start(f32[256,128]{1,0:T(8,128)S(1)} %get-tuple-element.33), channel_id=1, source_target_pairs={{0,24},{4,28},{8,0},{12,4},{16,8},{20,12},{24,16},{28,20},{1,25},{... | collective-permute-start | bytes 393224 | tf_op jit(solution)/shard_map/ppermute | solution.py:247
  691.5 15.6 %collective-permute-start.53 = (f32[256,128]{1,0:T(8,128)S(1)}, f32[256,128]{1,0:T(8,128)S(1)}, u32[]{:S(2)}, u32[]{:S(2)}) collective-permute-start(f32[256,128]{1,0:T(8,128)S(1)} %multiply_subtract_fusion.6), channel_id=1, source_target_pairs={{0,24},{4,28},{8,0},{12,4},{16,8},{20,12},{24,16},{28,20},{1,25},{... | collective-permute-start | bytes 393224 | tf_op jit(solution)/shard_map/ppermute | solution.py:257
  700.7 28.0 %collective-permute-start.54 = (f32[256,128]{1,0:T(8,128)S(1)}, f32[256,128]{1,0:T(8,128)S(1)}, u32[]{:S(2)}, u32[]{:S(2)}) collective-permute-start(f32[256,128]{1,0:T(8,128)S(1)} %multiply_subtract_fusion.6), channel_id=1, source_target_pairs={{0,16},{4,20},{8,24},{12,28},{16,0},{20,4},{24,8},{28,12},{1,17},{... | collective-permute-start | bytes 393224 | tf_op jit(solution)/shard_map/ppermute | solution.py:257
  700.7 28.0 %collective-permute-start.55 = (f32[256,128]{1,0:T(8,128)S(1)}, f32[256,128]{1,0:T(8,128)S(1)}, u32[]{:S(2)}, u32[]{:S(2)}) collective-permute-start(f32[256,128]{1,0:T(8,128)S(1)} %multiply_subtract_fusion.6), channel_id=1, source_target_pairs={{0,8},{4,12},{8,16},{12,20},{16,24},{20,28},{24,0},{28,4},{1,9},{5... | collective-permute-start | bytes 393224 | tf_op jit(solution)/shard_map/ppermute | solution.py:257
  701.5 27.4 %collective-permute-start.58 = (f32[320,128]{1,0:T(8,128)S(1)}, f32[320,128]{1,0:T(8,128)S(1)}, u32[]{:S(2)}, u32[]{:S(2)}) collective-permute-start(f32[320,128]{1,0:T(8,128)S(1)} %get-tuple-element.20), channel_id=1, source_target_pairs={{0,8},{4,12},{8,16},{12,20},{16,24},{20,28},{24,0},{28,4},{1,9},{5... | collective-permute-start | bytes 491528 | tf_op jit(solution)/shard_map/ppermute | solution.py:247
  704.4 35.4 %collective-permute-start.59 = (f32[320,128]{1,0:T(8,128)S(1)}, f32[320,128]{1,0:T(8,128)S(1)}, u32[]{:S(2)}, u32[]{:S(2)}) collective-permute-start(f32[320,128]{1,0:T(8,128)S(1)} %get-tuple-element.22), channel_id=1, source_target_pairs={{0,16},{4,20},{8,24},{12,28},{16,0},{20,4},{24,8},{28,12},{1,17},{... | collective-permute-start | bytes 491528 | tf_op jit(solution)/shard_map/ppermute | solution.py:247
  707.1 32.7 %collective-permute-start.60 = (f32[320,128]{1,0:T(8,128)S(1)}, f32[320,128]{1,0:T(8,128)S(1)}, u32[]{:S(2)}, u32[]{:S(2)}) collective-permute-start(f32[320,128]{1,0:T(8,128)S(1)} %get-tuple-element.21), channel_id=1, source_target_pairs={{0,24},{4,28},{8,0},{12,4},{16,8},{20,12},{24,16},{28,20},{1,25},{... | collective-permute-start | bytes 491528 | tf_op jit(solution)/shard_map/ppermute | solution.py:247
  739.8 15.6 %collective-permute-start.61 = (f32[320,128]{1,0:T(8,128)S(1)}, f32[320,128]{1,0:T(8,128)S(1)}, u32[]{:S(2)}, u32[]{:S(2)}) collective-permute-start(f32[320,128]{1,0:T(8,128)S(1)} %multiply_subtract_fusion.3), channel_id=1, source_target_pairs={{0,24},{4,28},{8,0},{12,4},{16,8},{20,12},{24,16},{28,20},{1,25},{... | collective-permute-start | bytes 491528 | tf_op jit(solution)/shard_map/ppermute | solution.py:257
  752.4 8.9 %collective-permute-start.62 = (f32[320,128]{1,0:T(8,128)S(1)}, f32[320,128]{1,0:T(8,128)S(1)}, u32[]{:S(2)}, u32[]{:S(2)}) collective-permute-start(f32[320,128]{1,0:T(8,128)S(1)} %multiply_subtract_fusion.3), channel_id=1, source_target_pairs={{0,16},{4,20},{8,24},{12,28},{16,0},{20,4},{24,8},{28,12},{1,17},{... | collective-permute-start | bytes 491528 | tf_op jit(solution)/shard_map/ppermute | solution.py:257
  752.9 14.9 %collective-permute-start.56 = (f32[1024,128]{1,0:T(8,128)S(1)}, f32[1024,128]{1,0:T(8,128)S(1)}, u32[]{:S(2)}, u32[]{:S(2)}) collective-permute-start(f32[1024,128]{1,0:T(8,128)S(1)} %constant_dynamic-slice_fusion.4), channel_id=1, source_target_pairs={{0,4},{4,0},{8,12},{12,8},{16,20},{20,16},{24,28},{28,24},{1,5},{5... | collective-permute-start | bytes 1572872 | tf_op jit(solution)/shard_map/ppermute | solution.py:257
  753.8 7.5 collective-permute-start.63
  761.5 14.5 %collective-permute-start.64 = (f32[1280,128]{1,0:T(8,128)S(1)}, f32[1280,128]{1,0:T(8,128)S(1)}, u32[]{:S(2)}, u32[]{:S(2)}) collective-permute-start(f32[1280,128]{1,0:T(8,128)S(1)} %constant_dynamic-slice_fusion.39), channel_id=1, source_target_pairs={{0,4},{4,0},{8,12},{12,8},{16,20},{20,16},{24,28},{28,24},{1,5},{5... | collective-permute-start | bytes 1966088 | tf_op jit(solution)/shard_map/ppermute | solution.py:257
  (42 other events, 693.7 us)
Sparse Core Ops, SparseCore 0:
  18.4 77.1 reduce-scatter.4
  99.1 84.5 reduce-scatter.6
  185.9 91.0 all-gather.3
  353.2 78.8 reduce-scatter.8
  434.2 75.8 all-gather.5
  589.2 73.1 reduce-scatter.10
  665.2 86.3 all-gather.7
